TPU v7x, 16 devices: a 4x2x1 block of a 4x4x8 slice. The times are simulated.
16 devices in a mesh: seqs: 2 (over y, z), states: 8 (over x, core).
Axes of the slice: x: 4, y: 2, z: 1, core: 2. Of those that a mesh axis runs over, the one named last changes fastest.
The devices are a block of a 4x4x8 slice.
Arguments:
- trans_mat: bfloat16 [16384, 16384], P(None, 'states')
- emit_mat: bfloat16 [16384, 10000], P('states')
- init_prob: float32 [16384], P('states')
- tokens: int32 [256, 16], P('seqs'), parts along dimension 0
- lengths: int32 [256], P('seqs'), parts along dimension 0
Outputs:
- output 1: float32 [256], P('seqs'), parts along dimension 0
- output 2: float32 [256, 16384], P('seqs', 'states'), parts along dimension 0
- output 3: float32 [32768, 2048], P(('seqs', 'states')), parts along dimension 0
There are 2 independent parts. A program takes and returns all parts, laid end to end along the dimension named above; an argument that names none is the same for every part.
All inputs are finite; a program needn't handle non-finite values.
Results may differ from a plain program's by a relative error of at most 0.001.
Values are sent between devices in bfloat16 or wider.
A program may use at most 768 MiB of HBM per device.

v0:
```python
import jax
import jax.numpy as jnp
from jax import lax
from jax.sharding import PartitionSpec as P


def solution(mesh):
    def step_weight(live_mask, emit_now, beta_cur, step_scale):
        scaled = emit_now.astype(jnp.float32) * beta_cur / step_scale[:, None]
        return jnp.where(live_mask[:, None], scaled, 0.0).astype(jnp.bfloat16)

    def local_run(trans_loc, emit_loc, init_loc, tokens_loc, lengths_loc):
        seq_count, step_count = tokens_loc.shape
        block_size = trans_loc.shape[1]
        group_idx = lax.axis_index('states')
        emit_seq = jnp.transpose(jnp.take(emit_loc, tokens_loc.T, axis=1), (1, 2, 0))
        first_mass = init_loc[None, :] * emit_seq[0].astype(jnp.float32)
        first_norm = lax.psum(jnp.sum(first_mass, axis=1), 'states')
        alpha_first = first_mass / first_norm[:, None]
        live_steps = jnp.arange(1, step_count)[:, None] < lengths_loc[None, :]

        def forward_step(alpha_cur, inputs):
            live_mask, emit_now = inputs
            alpha_bf = alpha_cur.astype(jnp.bfloat16)
            alpha_full = lax.all_gather(alpha_bf, 'states', axis=1, tiled=True)
            pred_mass = jnp.dot(alpha_full, trans_loc, preferred_element_type=jnp.float32)
            new_mass = pred_mass * emit_now.astype(jnp.float32)
            norm_sum = lax.psum(jnp.sum(new_mass, axis=1), 'states')
            step_scale = jnp.where(live_mask, norm_sum, 1.0)
            alpha_next = jnp.where(live_mask[:, None], new_mass / norm_sum[:, None], alpha_cur)
            return alpha_next, (alpha_bf, step_scale)

        alpha_last, (alpha_prev, scales) = lax.scan(forward_step, alpha_first, (live_steps, emit_seq[1:]))
        loglik = jnp.log(first_norm) + jnp.sum(jnp.log(scales), axis=0)

        def backward_step(beta_cur, inputs):
            live_mask, emit_now, step_scale = inputs
            weight = step_weight(live_mask, emit_now, beta_cur, step_scale)
            partial_sum = lax.dot_general(weight, trans_loc, (((1,), (1,)), ((), ())), preferred_element_type=jnp.float32)
            beta_prev = lax.psum_scatter(partial_sum, 'states', scatter_dimension=1, tiled=True)
            return beta_prev + jnp.where(live_mask, 0.0, 1.0)[:, None], weight

        beta_one, late_weights = lax.scan(backward_step, jnp.ones((seq_count, block_size), jnp.float32), (live_steps[1:], emit_seq[2:], scales[1:]), reverse=True)
        first_weight = step_weight(live_steps[0], emit_seq[1], beta_one, scales[0])
        pair_sum = jnp.einsum('tbi,tbj->ij', alpha_prev[1:], late_weights, preferred_element_type=jnp.float32)
        pair_sum = pair_sum + lax.dot_general(alpha_prev[0], first_weight, (((0,), (0,)), ((), ())), preferred_element_type=jnp.float32)
        diag_block = lax.dynamic_slice_in_dim(trans_loc, group_idx * block_size, block_size, axis=0)
        counts = diag_block.astype(jnp.float32) * pair_sum
        return loglik, alpha_last, counts

    return jax.shard_map(local_run, mesh=mesh, in_specs=(P(None, 'states'), P('states', None), P('states'), P('seqs', None), P('seqs')), out_specs=(P('seqs'), P('seqs', 'states'), P(('seqs', 'states'), None)), check_vma=False)
```

profile of v0, /device:TPU:112, one launch (start us, length us, event | category | flops | bytes accessed | tf_op | source)
XLA Modules:
  0.0 2295.0 jit_solution(1389716988372904941)
XLA Ops:
  7.9 47.9 %gather_fusion = bf16[2048,2048]{1,0:T(8,128)(2,1)} fusion(bf16[2048,10000]{0,1:T(8,128)(2,1)} %param.10, s32[2048]{0:T(1024)S(1)} %bitcast_clamp_fusion), kind=kCustom, calls=%fused_computation | custom fusion | bytes 16785408 | tf_op jit(solution)/shard_map/jit(_take)/gather | solution.py:16
  89.9 1019.4 %while.31 = (s32[]{:T(128)}, f32[128,2048]{1,0:T(8,128)S(1)}, bf16[15,128,2048]{2,1,0:T(8,128)(2,1)}, f32[15,128]{1,0:T(8,128)S(1)}, pred[15,128]{1,0:T(8,128)(4...) while((s32[]{:T(128)}, f32[128,2048]{1,0:T(8,128)S(1)}, ...), condition=%wide.region_5.6_spmd, body=%wide.region_2.0_spmd.sunk | while | flops 8591507456 | bytes 92279312 | solution.py:33
  1121.6 1127.6 %while.32 = (s32[]{:T(128)}, f32[128,2048]{1,0:T(8,128)S(1)}, bf16[14,128,2048]{2,1,0:T(8,128)(2,1)}, pred[14,128]{1,0:T(8,128)(4,1)S(1)}, bf16[14,128,2048]{2,1...) while((s32[]{:T(128)}, f32[128,2048]{1,0:T(8,128)S(1)}, ...), condition=%wide.region_9.10_spmd.clone, body=%wide.region_7.9_spmd.clone.sunk | while | flops 8593342464 | bytes 109579960 | solution.py:43
  1154.5 45.3 %reduce-scatter.2.cloned.1.call-done = f32[128,2048]{1,0:T(8,128)} async-done(((f32[128,16384]{1,0:T(8,128)}), f32[128,2048]{1,0:T(8,128)}) %reduce-scatter.2.cloned.1.call-update) | async-done | bytes 1048592 | tf_op jit(solution)/shard_map/while/body/eval_jaxpr/reduce_scatter | solution.py:40
  1201.3 30.8 %fusion.39 = f32[128,16384]{1,0:T(8,128)} fusion(bf16[16384,2048]{1,0:T(8,128)(2,1)} %get-tuple-element.404, f32[128,2048]{1,0:T(8,128)S(1)} %get-tuple-element.389, f32[128]{0:T(128)S(1)} %fusion.38, bf16[14,128,2048]{2,1,0:T(8,128)(2,1)} %get-tuple-element.402, s32[]{:T(128)S(6)} %sub.9, pred[128]{0:T(512)(128)(4,1)S(1)} %get-tuple-element.349, ...), kind=kOutput, calls=%fused_computation.16.clone.1 | convolution fusion | flops 8591507456 | bytes 77070984 | tf_op jit(solution)/shard_map/while/body/eval_jaxpr/dot_general | solution.py:39
  1234.3 46.1 %reduce-scatter.2.cloned.1.call-done = f32[128,2048]{1,0:T(8,128)} async-done(((f32[128,16384]{1,0:T(8,128)}), f32[128,2048]{1,0:T(8,128)}) %reduce-scatter.2.cloned.1.call-update) | async-done | bytes 1048592 | tf_op jit(solution)/shard_map/while/body/eval_jaxpr/reduce_scatter | solution.py:40
  1282.0 30.8 %fusion.39 = f32[128,16384]{1,0:T(8,128)} fusion(bf16[16384,2048]{1,0:T(8,128)(2,1)} %get-tuple-element.404, f32[128,2048]{1,0:T(8,128)S(1)} %get-tuple-element.389, f32[128]{0:T(128)S(1)} %fusion.38, bf16[14,128,2048]{2,1,0:T(8,128)(2,1)} %get-tuple-element.402, s32[]{:T(128)S(6)} %sub.9, pred[128]{0:T(512)(128)(4,1)S(1)} %get-tuple-element.349, ...), kind=kOutput, calls=%fused_computation.16.clone.1 | convolution fusion | flops 8591507456 | bytes 77070984 | tf_op jit(solution)/shard_map/while/body/eval_jaxpr/dot_general | solution.py:39
  1314.9 46.2 %reduce-scatter.2.cloned.1.call-done = f32[128,2048]{1,0:T(8,128)} async-done(((f32[128,16384]{1,0:T(8,128)}), f32[128,2048]{1,0:T(8,128)}) %reduce-scatter.2.cloned.1.call-update) | async-done | bytes 1048592 | tf_op jit(solution)/shard_map/while/body/eval_jaxpr/reduce_scatter | solution.py:40
  1362.6 30.8 %fusion.39 = f32[128,16384]{1,0:T(8,128)} fusion(bf16[16384,2048]{1,0:T(8,128)(2,1)} %get-tuple-element.404, f32[128,2048]{1,0:T(8,128)S(1)} %get-tuple-element.389, f32[128]{0:T(128)S(1)} %fusion.38, bf16[14,128,2048]{2,1,0:T(8,128)(2,1)} %get-tuple-element.402, s32[]{:T(128)S(6)} %sub.9, pred[128]{0:T(512)(128)(4,1)S(1)} %get-tuple-element.349, ...), kind=kOutput, calls=%fused_computation.16.clone.1 | convolution fusion | flops 8591507456 | bytes 77070984 | tf_op jit(solution)/shard_map/while/body/eval_jaxpr/dot_general | solution.py:39
  1395.5 46.2 %reduce-scatter.2.cloned.1.call-done = f32[128,2048]{1,0:T(8,128)} async-done(((f32[128,16384]{1,0:T(8,128)}), f32[128,2048]{1,0:T(8,128)}) %reduce-scatter.2.cloned.1.call-update) | async-done | bytes 1048592 | tf_op jit(solution)/shard_map/while/body/eval_jaxpr/reduce_scatter | solution.py:40
  1443.1 30.8 %fusion.39 = f32[128,16384]{1,0:T(8,128)} fusion(bf16[16384,2048]{1,0:T(8,128)(2,1)} %get-tuple-element.404, f32[128,2048]{1,0:T(8,128)S(1)} %get-tuple-element.389, f32[128]{0:T(128)S(1)} %fusion.38, bf16[14,128,2048]{2,1,0:T(8,128)(2,1)} %get-tuple-element.402, s32[]{:T(128)S(6)} %sub.9, pred[128]{0:T(512)(128)(4,1)S(1)} %get-tuple-element.349, ...), kind=kOutput, calls=%fused_computation.16.clone.1 | convolution fusion | flops 8591507456 | bytes 77070984 | tf_op jit(solution)/shard_map/while/body/eval_jaxpr/dot_general | solution.py:39
  1476.0 46.2 %reduce-scatter.2.cloned.1.call-done = f32[128,2048]{1,0:T(8,128)} async-done(((f32[128,16384]{1,0:T(8,128)}), f32[128,2048]{1,0:T(8,128)}) %reduce-scatter.2.cloned.1.call-update) | async-done | bytes 1048592 | tf_op jit(solution)/shard_map/while/body/eval_jaxpr/reduce_scatter | solution.py:40
  1556.7 46.2 %reduce-scatter.2.cloned.1.call-done = f32[128,2048]{1,0:T(8,128)} async-done(((f32[128,16384]{1,0:T(8,128)}), f32[128,2048]{1,0:T(8,128)}) %reduce-scatter.2.cloned.1.call-update) | async-done | bytes 1048592 | tf_op jit(solution)/shard_map/while/body/eval_jaxpr/reduce_scatter | solution.py:40
  1604.3 30.8 %fusion.39 = f32[128,16384]{1,0:T(8,128)} fusion(bf16[16384,2048]{1,0:T(8,128)(2,1)} %get-tuple-element.404, f32[128,2048]{1,0:T(8,128)S(1)} %get-tuple-element.389, f32[128]{0:T(128)S(1)} %fusion.38, bf16[14,128,2048]{2,1,0:T(8,128)(2,1)} %get-tuple-element.402, s32[]{:T(128)S(6)} %sub.9, pred[128]{0:T(512)(128)(4,1)S(1)} %get-tuple-element.349, ...), kind=kOutput, calls=%fused_computation.16.clone.1 | convolution fusion | flops 8591507456 | bytes 77070984 | tf_op jit(solution)/shard_map/while/body/eval_jaxpr/dot_general | solution.py:39
  1637.3 46.1 %reduce-scatter.2.cloned.1.call-done = f32[128,2048]{1,0:T(8,128)} async-done(((f32[128,16384]{1,0:T(8,128)}), f32[128,2048]{1,0:T(8,128)}) %reduce-scatter.2.cloned.1.call-update) | async-done | bytes 1048592 | tf_op jit(solution)/shard_map/while/body/eval_jaxpr/reduce_scatter | solution.py:40
  1684.9 30.8 %fusion.39 = f32[128,16384]{1,0:T(8,128)} fusion(bf16[16384,2048]{1,0:T(8,128)(2,1)} %get-tuple-element.404, f32[128,2048]{1,0:T(8,128)S(1)} %get-tuple-element.389, f32[128]{0:T(128)S(1)} %fusion.38, bf16[14,128,2048]{2,1,0:T(8,128)(2,1)} %get-tuple-element.402, s32[]{:T(128)S(6)} %sub.9, pred[128]{0:T(512)(128)(4,1)S(1)} %get-tuple-element.349, ...), kind=kOutput, calls=%fused_computation.16.clone.1 | convolution fusion | flops 8591507456 | bytes 77070984 | tf_op jit(solution)/shard_map/while/body/eval_jaxpr/dot_general | solution.py:39
  1717.9 46.2 %reduce-scatter.2.cloned.1.call-done = f32[128,2048]{1,0:T(8,128)} async-done(((f32[128,16384]{1,0:T(8,128)}), f32[128,2048]{1,0:T(8,128)}) %reduce-scatter.2.cloned.1.call-update) | async-done | bytes 1048592 | tf_op jit(solution)/shard_map/while/body/eval_jaxpr/reduce_scatter | solution.py:40
  1798.4 46.2 %reduce-scatter.2.cloned.1.call-done = f32[128,2048]{1,0:T(8,128)} async-done(((f32[128,16384]{1,0:T(8,128)}), f32[128,2048]{1,0:T(8,128)}) %reduce-scatter.2.cloned.1.call-update) | async-done | bytes 1048592 | tf_op jit(solution)/shard_map/while/body/eval_jaxpr/reduce_scatter | solution.py:40
  1879.1 46.1 %reduce-scatter.2.cloned.1.call-done = f32[128,2048]{1,0:T(8,128)} async-done(((f32[128,16384]{1,0:T(8,128)}), f32[128,2048]{1,0:T(8,128)}) %reduce-scatter.2.cloned.1.call-update) | async-done | bytes 1048592 | tf_op jit(solution)/shard_map/while/body/eval_jaxpr/reduce_scatter | solution.py:40
  1959.7 46.1 %reduce-scatter.2.cloned.1.call-done = f32[128,2048]{1,0:T(8,128)} async-done(((f32[128,16384]{1,0:T(8,128)}), f32[128,2048]{1,0:T(8,128)}) %reduce-scatter.2.cloned.1.call-update) | async-done | bytes 1048592 | tf_op jit(solution)/shard_map/while/body/eval_jaxpr/reduce_scatter | solution.py:40
  2007.3 30.8 %fusion.39 = f32[128,16384]{1,0:T(8,128)} fusion(bf16[16384,2048]{1,0:T(8,128)(2,1)} %get-tuple-element.404, f32[128,2048]{1,0:T(8,128)S(1)} %get-tuple-element.389, f32[128]{0:T(128)S(1)} %fusion.38, bf16[14,128,2048]{2,1,0:T(8,128)(2,1)} %get-tuple-element.402, s32[]{:T(128)S(6)} %sub.9, pred[128]{0:T(512)(128)(4,1)S(1)} %get-tuple-element.349, ...), kind=kOutput, calls=%fused_computation.16.clone.1 | convolution fusion | flops 8591507456 | bytes 77070984 | tf_op jit(solution)/shard_map/while/body/eval_jaxpr/dot_general | solution.py:39
  2040.2 46.2 %reduce-scatter.2.cloned.1.call-done = f32[128,2048]{1,0:T(8,128)} async-done(((f32[128,16384]{1,0:T(8,128)}), f32[128,2048]{1,0:T(8,128)}) %reduce-scatter.2.cloned.1.call-update) | async-done | bytes 1048592 | tf_op jit(solution)/shard_map/while/body/eval_jaxpr/reduce_scatter | solution.py:40
  2120.8 46.2 %reduce-scatter.2.cloned.1.call-done = f32[128,2048]{1,0:T(8,128)} async-done(((f32[128,16384]{1,0:T(8,128)}), f32[128,2048]{1,0:T(8,128)}) %reduce-scatter.2.cloned.1.call-update) | async-done | bytes 1048592 | tf_op jit(solution)/shard_map/while/body/eval_jaxpr/reduce_scatter | solution.py:40
  2201.4 46.2 %reduce-scatter.2.cloned.1.call-done = f32[128,2048]{1,0:T(8,128)} async-done(((f32[128,16384]{1,0:T(8,128)}), f32[128,2048]{1,0:T(8,128)}) %reduce-scatter.2.cloned.1.call-update) | async-done | bytes 1048592 | tf_op jit(solution)/shard_map/while/body/eval_jaxpr/reduce_scatter | solution.py:40
  (256 shorter events, 1370.4 us)
Async XLA Ops:
  89.9 30.1 %all-gather.2.cloned.1.call-start = ((), (), s32[]{:S(2)}) async-start(), calls=%async_computation.1 | async-start | bytes 4718592 | tf_op jit(solution)/shard_map/while/body/eval_jaxpr/all_gather | solution.py:25
  158.5 29.6 %all-gather.2.cloned.1.call-start = ((), (), s32[]{:S(2)}) async-start(), calls=%async_computation.1 | async-start | bytes 4718592 | tf_op jit(solution)/shard_map/while/body/eval_jaxpr/all_gather | solution.py:25
  226.6 29.6 %all-gather.2.cloned.1.call-start = ((), (), s32[]{:S(2)}) async-start(), calls=%async_computation.1 | async-start | bytes 4718592 | tf_op jit(solution)/shard_map/while/body/eval_jaxpr/all_gather | solution.py:25
  497.9 29.6 %all-gather.2.cloned.1.call-start = ((), (), s32[]{:S(2)}) async-start(), calls=%async_computation.1 | async-start | bytes 4718592 | tf_op jit(solution)/shard_map/while/body/eval_jaxpr/all_gather | solution.py:25
  566.0 29.6 %all-gather.2.cloned.1.call-start = ((), (), s32[]{:S(2)}) async-start(), calls=%async_computation.1 | async-start | bytes 4718592 | tf_op jit(solution)/shard_map/while/body/eval_jaxpr/all_gather | solution.py:25
  634.0 29.6 %all-gather.2.cloned.1.call-start = ((), (), s32[]{:S(2)}) async-start(), calls=%async_computation.1 | async-start | bytes 4718592 | tf_op jit(solution)/shard_map/while/body/eval_jaxpr/all_gather | solution.py:25
  702.1 29.2 %all-gather.2.cloned.1.call-start = ((), (), s32[]{:S(2)}) async-start(), calls=%async_computation.1 | async-start | bytes 4718592 | tf_op jit(solution)/shard_map/while/body/eval_jaxpr/all_gather | solution.py:25
  769.9 29.6 %all-gather.2.cloned.1.call-start = ((), (), s32[]{:S(2)}) async-start(), calls=%async_computation.1 | async-start | bytes 4718592 | tf_op jit(solution)/shard_map/while/body/eval_jaxpr/all_gather | solution.py:25
  905.7 29.6 %all-gather.2.cloned.1.call-start = ((), (), s32[]{:S(2)}) async-start(), calls=%async_computation.1 | async-start | bytes 4718592 | tf_op jit(solution)/shard_map/while/body/eval_jaxpr/all_gather | solution.py:25
  1041.5 29.2 %all-gather.2.cloned.1.call-start = ((), (), s32[]{:S(2)}) async-start(), calls=%async_computation.1 | async-start | bytes 4718592 | tf_op jit(solution)/shard_map/while/body/eval_jaxpr/all_gather | solution.py:25
  1121.6 78.2 %reduce-scatter.2.cloned.1.call-start = ((), (), s32[]{:S(2)}) async-start(), calls=%async_computation.2 | async-start | bytes 9437184 | tf_op jit(solution)/shard_map/while/body/eval_jaxpr/reduce_scatter | solution.py:40
  1201.2 79.3 %reduce-scatter.2.cloned.1.call-start = ((), (), s32[]{:S(2)}) async-start(), calls=%async_computation.2 | async-start | bytes 9437184 | tf_op jit(solution)/shard_map/while/body/eval_jaxpr/reduce_scatter | solution.py:40
  1281.8 79.2 %reduce-scatter.2.cloned.1.call-start = ((), (), s32[]{:S(2)}) async-start(), calls=%async_computation.2 | async-start | bytes 9437184 | tf_op jit(solution)/shard_map/while/body/eval_jaxpr/reduce_scatter | solution.py:40
  1362.4 79.2 %reduce-scatter.2.cloned.1.call-start = ((), (), s32[]{:S(2)}) async-start(), calls=%async_computation.2 | async-start | bytes 9437184 | tf_op jit(solution)/shard_map/while/body/eval_jaxpr/reduce_scatter | solution.py:40
  1443.0 79.2 %reduce-scatter.2.cloned.1.call-start = ((), (), s32[]{:S(2)}) async-start(), calls=%async_computation.2 | async-start | bytes 9437184 | tf_op jit(solution)/shard_map/while/body/eval_jaxpr/reduce_scatter | solution.py:40
  1523.6 79.2 %reduce-scatter.2.cloned.1.call-start = ((), (), s32[]{:S(2)}) async-start(), calls=%async_computation.2 | async-start | bytes 9437184 | tf_op jit(solution)/shard_map/while/body/eval_jaxpr/reduce_scatter | solution.py:40
  1604.2 79.2 %reduce-scatter.2.cloned.1.call-start = ((), (), s32[]{:S(2)}) async-start(), calls=%async_computation.2 | async-start | bytes 9437184 | tf_op jit(solution)/shard_map/while/body/eval_jaxpr/reduce_scatter | solution.py:40
  1684.8 79.2 %reduce-scatter.2.cloned.1.call-start = ((), (), s32[]{:S(2)}) async-start(), calls=%async_computation.2 | async-start | bytes 9437184 | tf_op jit(solution)/shard_map/while/body/eval_jaxpr/reduce_scatter | solution.py:40
  1765.4 79.2 %reduce-scatter.2.cloned.1.call-start = ((), (), s32[]{:S(2)}) async-start(), calls=%async_computation.2 | async-start | bytes 9437184 | tf_op jit(solution)/shard_map/while/body/eval_jaxpr/reduce_scatter | solution.py:40
  1846.0 79.2 %reduce-scatter.2.cloned.1.call-start = ((), (), s32[]{:S(2)}) async-start(), calls=%async_computation.2 | async-start | bytes 9437184 | tf_op jit(solution)/shard_map/while/body/eval_jaxpr/reduce_scatter | solution.py:40
  1926.6 79.2 %reduce-scatter.2.cloned.1.call-start = ((), (), s32[]{:S(2)}) async-start(), calls=%async_computation.2 | async-start | bytes 9437184 | tf_op jit(solution)/shard_map/while/body/eval_jaxpr/reduce_scatter | solution.py:40
  2007.2 79.2 %reduce-scatter.2.cloned.1.call-start = ((), (), s32[]{:S(2)}) async-start(), calls=%async_computation.2 | async-start | bytes 9437184 | tf_op jit(solution)/shard_map/while/body/eval_jaxpr/reduce_scatter | solution.py:40
  2087.8 79.2 %reduce-scatter.2.cloned.1.call-start = ((), (), s32[]{:S(2)}) async-start(), calls=%async_computation.2 | async-start | bytes 9437184 | tf_op jit(solution)/shard_map/while/body/eval_jaxpr/reduce_scatter | solution.py:40
  2168.4 79.2 %reduce-scatter.2.cloned.1.call-start = ((), (), s32[]{:S(2)}) async-start(), calls=%async_computation.2 | async-start | bytes 9437184 | tf_op jit(solution)/shard_map/while/body/eval_jaxpr/reduce_scatter | solution.py:40
  (9 other events, 228.6 us)
Sparse Core Ops, SparseCore 0:
  92.8 27.1 all-gather.1
  161.5 26.5 all-gather.1
  229.6 26.5 all-gather.1
  297.3 26.5 all-gather.1
  500.9 26.5 all-gather.1
  569.0 26.5 all-gather.1
  637.0 26.5 all-gather.1
  840.6 26.5 all-gather.1
  976.4 26.5 all-gather.1
  1044.2 26.5 all-gather.1
  1152.6 47.1 reduce-scatter.1
  1232.3 48.0 reduce-scatter.1
  1312.9 48.0 reduce-scatter.1
  1393.5 48.0 reduce-scatter.1
  1474.1 48.0 reduce-scatter.1
  1554.7 48.0 reduce-scatter.1
  1635.3 48.0 reduce-scatter.1
  1715.9 48.0 reduce-scatter.1
  1796.5 48.0 reduce-scatter.1
  1877.1 48.0 reduce-scatter.1
  1957.7 48.0 reduce-scatter.1
  2038.3 48.0 reduce-scatter.1
  2118.9 48.0 reduce-scatter.1
  2199.5 48.0 reduce-scatter.1
  (5 shorter events, 132.3 us)
where the time goes:
time: 2300 us
  waiting for transfers between devices  1070 us (47%)
  matrix products  846 us (37%)
  blocking collectives  213 us (9%)
  other arithmetic  79.8 us (3%)
  local copies, waits for them, and re-layouts  68.4 us (3%)
    reduce_scatter x14, waiting for transfers between devices, backward_step(): lax.psum_scatter(partial_sum, 'states', scatter_dimension=1, tiled=True)  645 us
    dot_general x14, matrix products, backward_step(): lax.dot_general(weight, trans_loc, (((1,), (1,)), ((), ())), preferred_el...  431 us
    all_gather x15, waiting for transfers between devices, forward_step(): alpha_full = lax.all_gather(alpha_bf, 'states', axis=1, tiled=True)  423 us
    dot_general x15, matrix products, forward_step(): jnp.dot(alpha_full, trans_loc, preferred_element_type=jnp.float32)  376 us
    psum x15, blocking collectives, forward_step(): norm_sum = lax.psum(jnp.sum(new_mass, axis=1), 'states')  197 us
    gather x1, local copies, waits for them, and re-layouts, local_run(): jnp.take(emit_loc, tokens_loc.T, axis=1)  47.9 us
  transfers between devices with their start and end apart: 29, of which 29 were waited for; matrix products, arithmetic and copies ran while one was open for 1% of the time, Pallas kernels for 0%

commit v1 on v0

v1 whole, which is shorter than its diff:
```python
import functools

import jax
import jax.numpy as jnp
from jax import lax
from jax.experimental import pallas as pl
from jax.experimental.pallas import tpu as pltpu
from jax.sharding import PartitionSpec as P

MESH = pl.DeviceIdType.MESH
ANY = pl.BlockSpec(memory_space=pl.ANY)
VMEM = pl.BlockSpec(memory_space=pltpu.VMEM)
LANES = 128


def _place(n):
    me = lax.axis_index('states')
    core = lax.rem(me, 2)
    chip = lax.div(me, 2)
    partner = chip * 2 + (1 - core)
    right = lax.rem(me + 2, n)
    left = lax.rem(me + n - 2, n)
    return me, chip, core, partner, right, left


def _dev(peer):
    return {'states': peer}


def _barrier(me, n):
    barrier = pltpu.get_barrier_semaphore()
    for r in range(1, n):
        pl.semaphore_signal(barrier, inc=1, device_id=_dev(lax.rem(me + r, n)), device_id_type=MESH)
    pl.semaphore_wait(barrier, n - 1)


def _remote(src, dst, ssem, rsem, peer):
    return pltpu.make_async_remote_copy(src_ref=src, dst_ref=dst, send_sem=ssem, recv_sem=rsem, device_id=_dev(peer), device_id_type=MESH)


def _fwd_kernel(n, steps, rows, nbuf, a_hbm, e_hbm, pi_ref, code_ref, al_hbm, x_hbm, cc_ref,
                g, w, u, al, ebuf, tbuf, cs_send, cs_recv,
                e_sem, w_sem, r_sem, out_sem, cs_ss, cs_rs, own_ss, own_rs, ici_ss, ici_rs, dd_ss, dd_rs):
    me, chip, core, partner, right, left = _place(n)
    chips = n // 2
    half = a_hbm.shape[0] // (2 * n)
    wide = 2 * half
    nq = wide // LANES
    total = (steps - 1) * 8

    def chip_off(j, i):
        mid = jnp.where(i == 0, chips - 1, 1)
        return jnp.where(j == 0, 0, jnp.where(j == 3, 2, mid))

    def block(j, cls, i):
        hh = jnp.where(j == 2, 1 - i, i)
        c = lax.rem(chip + chip_off(j, i), chips)
        k = jnp.where(cls == 0, core, 1 - core)
        return (c * 2 + k) * 2 + hh

    def stream(q, slot):
        k = lax.rem(q, 8)
        b = block(lax.div(k, 2), 1, lax.rem(k, 2))
        return pltpu.make_async_copy(a_hbm.at[pl.ds(pl.multiple_of(b * half, half), half), :], w.at[8 + slot], w_sem.at[slot])

    def resident(k):
        b = block(jnp.int32(k // 2), 0, jnp.int32(k % 2))
        return pltpu.make_async_copy(a_hbm.at[pl.ds(pl.multiple_of(b * half, half), half), :], w.at[k], r_sem.at[k])

    def e_copy(s):
        return pltpu.make_async_copy(e_hbm.at[s], ebuf.at[lax.rem(s, 2)], e_sem.at[lax.rem(s, 2)])

    e_copy(jnp.int32(0)).start()
    for k in range(8):
        resident(k).start()
    for q in range(nbuf):
        stream(jnp.int32(q), q).start()
    tbuf[...] = jnp.zeros_like(tbuf)
    u[...] = jnp.zeros_like(u)
    _barrier(me, n)

    def al_copy(s):
        return pltpu.make_async_copy(al, al_hbm.at[s], out_sem.at[2])

    def x_copy(s, h):
        return pltpu.make_async_copy(g.at[me * 2 + h], x_hbm.at[s, :, pl.ds(h * half, half)], out_sem.at[h])

    def own_sends():
        h0, h1 = g.at[me * 2], g.at[me * 2 + 1]
        return [
            _remote(h0, h0, ici_ss.at[0], ici_rs.at[0], right),
            _remote(h1, h1, ici_ss.at[1], ici_rs.at[1], left),
            _remote(h0, h0, dd_ss.at[0], dd_rs.at[0], partner),
            _remote(h1, h1, dd_ss.at[1], dd_rs.at[1], partner),
            _remote(h1, h1, ici_ss.at[2], ici_rs.at[2], right),
            _remote(h0, h0, ici_ss.at[3], ici_rs.at[3], left),
        ]

    def ici_wait(j, i):
        ref = g.at[block(j, 0, i)]
        k = (j - 1) * 2 + i
        _remote(ref, ref, ici_ss.at[k], ici_rs.at[k], left).wait_recv()

    def dd(j, i, k):
        ref = g.at[block(j, 0, i)]
        return _remote(ref, ref, dd_ss.at[k], dd_rs.at[k], partner)

    def relay(i):
        ref = g.at[block(jnp.int32(1), 0, i)]
        return _remote(ref, ref, ici_ss.at[4 + i], ici_rs.at[4 + i], right if i == 0 else left)

    def step(s, _):
        e_copy(s).wait()

        @pl.when(s + 1 < steps)
        def _():
            e_copy(s + 1).start()

        @pl.when(s > 0)
        def _():
            al_copy(s - 1).wait()

        code = code_ref[s]
        init = (code > 0.5) & (code < 2.5)
        part = jnp.zeros((rows, LANES), jnp.float32)
        eb = ebuf.at[lax.rem(s, 2)]
        for q in range(nq):
            cols = slice(q * LANES, (q + 1) * LANES)
            mass = jnp.where(init, jnp.broadcast_to(pi_ref[:, cols], (rows, LANES)), u[:, cols])
            a = mass * eb[:, cols].astype(jnp.float32)
            al[:, cols] = a
            part = part + a
        tbuf[0:rows, :] = part
        row = jnp.sum(tbuf[...].T, axis=0, keepdims=True)
        cs_send[...] = jnp.broadcast_to(row, cs_send.shape)
        cs_recv[me] = jnp.broadcast_to(row, cs_send.shape)
        cps = []
        for r in (4, 3, 5, 2, 6, 1, 7):
            cp = _remote(cs_send, cs_recv.at[me], cs_ss.at[r - 1], cs_rs.at[r - 1], lax.rem(me + r, n))
            cp.start()
            cps.append(cp)

        @pl.when(s > 0)
        def _():
            for h in range(2):
                x_copy(s - 1, h).wait()

        for cp in cps:
            cp.wait()
        crow = cs_recv[0]
        for r in range(1, n):
            crow = crow + cs_recv[r]
        ccol = jnp.broadcast_to(crow[0:1, :], (LANES, LANES)).T[0:rows, :]
        cc_ref[s] = ccol
        live = code > 0.5
        safe = jnp.where(live, ccol, 1.0)
        for q in range(nq):
            cols = slice(q * LANES, (q + 1) * LANES)
            alpha = jnp.where(live, al[:, cols] / safe, 0.0)
            al[:, cols] = alpha
            h, o = divmod(q * LANES, half)
            g[me * 2 + h, :, o:o + LANES] = alpha.astype(jnp.bfloat16)
        al_copy(s).start()
        for h in range(2):
            x_copy(s, h).start()

        @pl.when(s + 1 < steps)
        def _():
            sends = own_sends()
            for cp in sends:
                cp.start()

            def rounds(j, _):
                @pl.when(j > 0)
                def _():
                    for i in range(2):
                        ici_wait(j, jnp.int32(i))

                    @pl.when(j == 1)
                    def _():
                        for i in range(2):
                            relay(i).start()

                    for i in range(2):
                        dd(j, jnp.int32(i), 2 * j + i).start()

                @pl.when(s == 0)
                def _():
                    for i in range(2):
                        ref = w.at[2 * j + i]
                        pltpu.make_async_copy(ref, ref, r_sem.at[2 * j + i]).wait()

                b0, b1 = block(j, jnp.int32(0), 0), block(j, jnp.int32(0), 1)
                prod = jnp.dot(g[b0], w[2 * j], preferred_element_type=jnp.float32)
                prod = prod + jnp.dot(g[b1], w[2 * j + 1], preferred_element_type=jnp.float32)

                @pl.when(j == 0)
                def _():
                    u[...] = prod

                @pl.when(j > 0)
                def _():
                    u[...] += prod

                for i in range(2):
                    k = 2 * j + i
                    ref = g.at[block(j, jnp.int32(1), i)]
                    _remote(ref, ref, dd_ss.at[k], dd_rs.at[k], partner).wait_recv()
                b0, b1 = block(j, jnp.int32(1), 0), block(j, jnp.int32(1), 1)
                q0 = s * 8 + 2 * j
                s0, s1 = lax.rem(q0, nbuf), lax.rem(q0 + 1, nbuf)
                stream(q0, s0).wait()
                stream(q0 + 1, s1).wait()
                u[...] += jnp.dot(g[b0], w[8 + s0], preferred_element_type=jnp.float32) + jnp.dot(
                    g[b1], w[8 + s1], preferred_element_type=jnp.float32)

                @pl.when(q0 + nbuf < total)
                def _():
                    stream(q0 + nbuf, s0).start()

                @pl.when(q0 + 1 + nbuf < total)
                def _():
                    stream(q0 + 1 + nbuf, s1).start()

                return 0

            lax.fori_loop(0, 4, rounds, 0)
            for cp in sends:
                cp.wait_send()
            for i in range(2):
                relay(i).wait_send()
            for j in range(1, 4):
                for i in range(2):
                    dd(jnp.int32(j), jnp.int32(i), 2 * j + i).wait_send()

        return 0

    lax.fori_loop(0, steps, step, 0)
    al_copy(steps - 1).wait()
    for h in range(2):
        x_copy(steps - 1, h).wait()


def _forward(n, a_loc, e_seq, init_loc, code):
    steps, rows, wide = e_seq.shape
    half = wide // 2
    nbuf = 4 if rows <= 80 else 2
    f32, bf16 = jnp.float32, jnp.bfloat16
    dma = pltpu.SemaphoreType.DMA
    return pl.pallas_call(
        functools.partial(_fwd_kernel, n, steps, rows, nbuf),
        out_shape=(
            jax.ShapeDtypeStruct((steps, rows, wide), f32),
            jax.ShapeDtypeStruct((steps, rows, wide), bf16),
            jax.ShapeDtypeStruct((steps, rows, LANES), f32),
        ),
        in_specs=[ANY, ANY, VMEM, VMEM],
        out_specs=(ANY, ANY, VMEM),
        scratch_shapes=[
            pltpu.VMEM((2 * n, rows, half), bf16),
            pltpu.VMEM((8 + nbuf, half, wide), bf16),
            pltpu.VMEM((rows, wide), f32),
            pltpu.VMEM((rows, wide), f32),
            pltpu.VMEM((2, rows, wide), bf16),
            pltpu.VMEM((LANES, LANES), f32),
            pltpu.VMEM((8, LANES), f32),
            pltpu.VMEM((n, 8, LANES), f32),
            dma((2,)), dma((nbuf,)), dma((8,)), dma((3,)),
            dma((n - 1,)), dma((n - 1,)),
            dma((2,)), dma((2,)),
            dma((6,)), dma((6,)), dma((8,)), dma((8,)),
        ],
        compiler_params=pltpu.CompilerParams(collective_id=0, has_side_effects=True, vmem_limit_bytes=67043328),
        name='forward',
    )(a_loc, e_seq, init_loc, code)


def _bwd_kernel(n, steps, rows, nbuf, a_hbm, e_hbm, cc_ref, code_ref, w_hbm,
                w, wv, beta, ebuf, pp, rp, rs, rin,
                e_sem, w_sem, r_sem, out_sem, dd_ss, dd_rs, ici_ss, ici_rs):
    me, chip, core, partner, right, left = _place(n)
    chips = n // 2
    half = a_hbm.shape[0] // (2 * n)
    wide = 2 * half
    nq = wide // LANES
    rounds_n = steps - 2
    total = rounds_n * 8

    def block(j, cls, i):
        hh = jnp.where(j == 1, 1 - i, i)
        mid = jnp.where(i == 0, 1, chips - 1)
        off = jnp.where(j == 0, 2, jnp.where(j == 3, 0, mid))
        c = lax.rem(chip + off, chips)
        k = jnp.where(cls == 0, core, 1 - core)
        return (c * 2 + k) * 2 + hh

    def stream(q, slot):
        k = lax.rem(q, 8)
        b = block(lax.div(k, 2), 1, lax.rem(k, 2))
        return pltpu.make_async_copy(a_hbm.at[pl.ds(pl.multiple_of(b * half, half), half), :], w.at[8 + slot], w_sem.at[slot])

    def resident(k):
        b = block(jnp.int32(k // 2), 0, jnp.int32(k % 2))
        return pltpu.make_async_copy(a_hbm.at[pl.ds(pl.multiple_of(b * half, half), half), :], w.at[k], r_sem.at[k])

    def e_copy(t):
        return pltpu.make_async_copy(e_hbm.at[steps - 1 - t], ebuf.at[lax.rem(t, 2)], e_sem.at[lax.rem(t, 2)])

    def w_copy(t):
        return pltpu.make_async_copy(wv, w_hbm.at[steps - 1 - t], out_sem)

    e_copy(jnp.int32(0)).start()
    for q in range(nbuf):
        stream(jnp.int32(q), q).start()
    for k in range(8):
        resident(k).start()
    _barrier(me, n)

    def nt(x, m):
        return lax.dot_general(x, m, (((1,), (1,)), ((), ())), preferred_element_type=jnp.float32)

    def dd(k):
        return _remote(pp.at[k], rp.at[k], dd_ss.at[k], dd_rs.at[k], partner)

    def ring(k, par, peer):
        return _remote(rs.at[k], rin.at[par, k], ici_ss.at[k], ici_rs.at[par, k], peer)

    def weights(t):
        s = steps - 1 - t
        e_copy(t).wait()

        @pl.when(t + 1 < steps - 1)
        def _():
            e_copy(t + 1).start()

        @pl.when(t > 0)
        def _():
            w_copy(t - 1).wait()

        code = code_ref[s]
        last = code > 3.5
        ok = code > 2.5
        safe = jnp.where(ok, cc_ref[s], 1.0)
        eb = ebuf.at[lax.rem(t, 2)]
        for q in range(nq):
            cols = slice(q * LANES, (q + 1) * LANES)
            b = jnp.where(last, 1.0, beta[:, cols])
            v = eb[:, cols].astype(jnp.float32) * b / safe
            wv[:, cols] = jnp.where(ok, v, 0.0).astype(jnp.bfloat16)
        w_copy(t).start()

    def step(t, _):
        par = lax.rem(t, 2)
        weights(t)

        def rounds(j, _):
            for i in range(2):
                k = 2 * j + i
                q = t * 8 + k
                slot = lax.rem(q, nbuf)
                stream(q, slot).wait()

                @pl.when(t > 0)
                def _():
                    dd(k).wait_send()

                pp[k] = nt(wv[...], w[8 + slot])
                dd(k).start()

                @pl.when(q + nbuf < total)
                def _():
                    stream(q + nbuf, slot).start()

            for i in range(2):
                k = 2 * j + i

                @pl.when(t == 0)
                def _():
                    ref = w.at[k]
                    pltpu.make_async_copy(ref, ref, r_sem.at[k]).wait()

                prod = nt(wv[...], w[k])
                dd(k).wait_recv()

                @pl.when(j < 3)
                def _():
                    @pl.when(t > 0)
                    def _():
                        ring(k, par, right if i == 0 else left).wait_send()

                    @pl.when(j < 2)
                    def _():
                        rs[k] = prod + rp[k]

                    @pl.when(j == 2)
                    def _():
                        ring(i, par, right if i == 0 else left).wait_recv()
                        rs[k] = prod + rp[k] + rin[par, i]

                    ring(k, par, right if i == 0 else left).start()

                @pl.when(j == 3)
                def _():
                    beta[:, i * half:(i + 1) * half] = prod + rp[k]

            return 0

        lax.fori_loop(0, 4, rounds, 0)
        for k, h in ((2, 1), (3, 0), (4, 0), (5, 1)):
            ring(k, par, right).wait_recv()
            beta[:, h * half:(h + 1) * half] += rin[par, k]
        return 0

    lax.fori_loop(0, rounds_n, step, 0)
    weights(jnp.int32(rounds_n))
    w_copy(rounds_n).wait()
    for k in range(8):
        dd(k).wait_send()
    for k in range(6):
        ring(k, 0, right).wait_send()


def _backward(n, a_loc, e_seq, ccol, code):
    steps, rows, wide = e_seq.shape
    half = wide // 2
    nbuf = 3 if rows <= 80 else 2
    f32, bf16 = jnp.float32, jnp.bfloat16
    dma = pltpu.SemaphoreType.DMA
    return pl.pallas_call(
        functools.partial(_bwd_kernel, n, steps, rows, nbuf),
        out_shape=jax.ShapeDtypeStruct((steps, rows, wide), bf16),
        in_specs=[ANY, ANY, VMEM, VMEM],
        out_specs=ANY,
        scratch_shapes=[
            pltpu.VMEM((8 + nbuf, half, wide), bf16),
            pltpu.VMEM((rows, wide), bf16),
            pltpu.VMEM((rows, wide), f32),
            pltpu.VMEM((2, rows, wide), bf16),
            pltpu.VMEM((8, rows, half), f32),
            pltpu.VMEM((8, rows, half), f32),
            pltpu.VMEM((6, rows, half), f32),
            pltpu.VMEM((2, 6, rows, half), f32),
            dma((2,)), dma((nbuf,)), dma((8,)), dma(()),
            dma((8,)), dma((8,)),
            dma((6,)), dma((2, 6)),
        ],
        compiler_params=pltpu.CompilerParams(collective_id=1, has_side_effects=True, vmem_limit_bytes=67043328),
        name='backward',
    )(a_loc, e_seq, ccol, code)


def solution(mesh):
    n = mesh.shape['states']

    def local_run(trans_loc, emit_loc, init_loc, tokens_loc, lengths_loc):
        rows, steps = tokens_loc.shape
        wide = trans_loc.shape[1]
        group_idx = lax.axis_index('states')
        pos = jnp.arange(steps, dtype=jnp.int32)[:, None]
        tok = tokens_loc.T
        init = pos == 0
        live = pos < lengths_loc[None, :]
        last = pos == lengths_loc[None, :] - 1
        code = jnp.where(live, jnp.where(init, 1.0, 3.0) + jnp.where(last, 1.0, 0.0), 0.0)
        code_b = jnp.broadcast_to(code[:, :, None], (steps, rows, LANES))
        e_seq = jnp.transpose(jnp.take(emit_loc, tok, axis=1), (1, 2, 0))
        al, xs, ccol = _forward(n, trans_loc, e_seq, init_loc[None, :], code_b)
        ws = _backward(n, trans_loc, e_seq, ccol, code_b)
        cc = ccol[:, :, 0]
        loglik = jnp.sum(jnp.where(live, jnp.log(jnp.where(live, cc, 1.0)), 0.0), axis=0)
        seq = jnp.arange(rows, dtype=jnp.int32)
        posterior = al.reshape(steps * rows, wide)[(lengths_loc - 1) * rows + seq]
        pair_sum = jnp.einsum('tbi,tbj->ij', xs[:-1], ws[1:], preferred_element_type=jnp.float32)
        diag_block = lax.dynamic_slice_in_dim(trans_loc, group_idx * wide, wide, axis=0)
        counts = diag_block.astype(jnp.float32) * pair_sum
        return loglik, posterior, counts

    return jax.shard_map(local_run, mesh=mesh, in_specs=(P(None, 'states'), P('states', None), P('states'), P('seqs', None), P('seqs')), out_specs=(P('seqs'), P('seqs', 'states'), P(('seqs', 'states'), None)), check_vma=False)
```

time: 2300 us -> 1100 us (0.48)
  waiting for transfers between devices: 1070 us -> 0 us
  Pallas kernels: 0 us -> 1000 us
  matrix products: 846 us -> 24.9 us
  blocking collectives: 213 us -> 0 us
  other arithmetic: 79.8 us -> 10.8 us
    pallas_call x0 -> x2, Pallas kernels: none -> 1000 us  [the longest x1 592 us: _backward(): pl.pallas_call(functools.partial(_bwd_kernel, n, steps, rows, nbuf), out_...]
    dot_general x31 -> x1, matrix products: 846 us -> 24.9 us  [local_run(): jnp.einsum('tbi,tbj->ij', xs[:-1], ws[1:], preferred_element_type=jnp.flo...]
    reduce_scatter x14 -> x0, waiting for transfers between devices: 645 us -> none  [backward_step(): lax.psum_scatter(partial_sum, 'states', scatter_dimension=1, tiled=True)]
    all_gather x15 -> x0, waiting for transfers between devices: 423 us -> none  [forward_step(): alpha_full = lax.all_gather(alpha_bf, 'states', axis=1, tiled=True)]
    psum x16 -> x0, blocking collectives: 213 us -> none  [the longest x15 197 us: forward_step(): norm_sum = lax.psum(jnp.sum(new_mass, axis=1), 'states')]
    dynamic_update_slice x29 -> x0, other arithmetic: 45.9 us -> none  [the longest x14 29 us: local_run(): lax.scan(backward_step, jnp.ones((seq_count, block_size), jnp.float32), (...]
    gather x1 -> x2, local copies, waits for them, and re-layouts: 47.9 us -> 56.1 us  [the longest x1 47.9 us: local_run(): e_seq = jnp.transpose(jnp.take(emit_loc, tok, axis=1), (1, 2, 0))]
  transfers between devices with their start and end apart: 29 -> 0, of which waited for: 29 -> 0; matrix products, arithmetic and copies ran while one was open for 1% -> 0% of each run, Pallas kernels for 0% -> 0%
where the time goes in v1:
time: 1100 us
  Pallas kernels  1000 us (91%)
  local copies, waits for them, and re-layouts  59.1 us (5%)
  matrix products  24.9 us (2%)
    pallas_call x1, Pallas kernels, _backward(): pl.pallas_call(functools.partial(_bwd_kernel, n, steps, rows, nbuf), out_...  592 us
    pallas_call x1, Pallas kernels, _forward(): pl.pallas_call(functools.partial(_fwd_kernel, n, steps, rows, nbuf), out_...  409 us
    gather x1, local copies, waits for them, and re-layouts, local_run(): e_seq = jnp.transpose(jnp.take(emit_loc, tok, axis=1), (1, 2, 0))  47.9 us
    dot_general x1, matrix products, local_run(): jnp.einsum('tbi,tbj->ij', xs[:-1], ws[1:], preferred_element_type=jnp.flo...  24.9 us

profile of v1, /device:TPU:112, one launch (start us, length us, event | category | flops | bytes accessed | tf_op | source)
XLA Modules:
  0.0 1097.2 jit_solution(4669290823427579297)
XLA Ops:
  0.6 0.7 bitcast_clamp_fusion
  1.3 0.0 copy-start
  1.3 47.9 %gather_fusion = bf16[2048,2048]{1,0:T(8,128)(2,1)} fusion(bf16[2048,10000]{0,1:T(8,128)(2,1)} %param.6, s32[2048]{0:T(1024)S(1)} %bitcast_clamp_fusion), kind=kCustom, calls=%fused_computation | custom fusion | bytes 16785408 | tf_op jit(solution)/shard_map/jit(_take)/gather | solution.py:466
  49.3 0.0 copy-done
  49.3 0.0 copy-start.1
  49.3 7.6 broadcast_select_fusion.e_hbm
  56.9 0.0 copy-done.1
  56.9 0.5 compare_select_fusion.1
  57.5 0.1 add_select_fusion
  57.5 1.4 broadcast_in_dim.56.code_ref
  58.9 409.5 %forward.1 = (f32[16,128,2048]{2,1,0:T(8,128)}, bf16[16,128,2048]{2,1,0:T(8,128)(2,1)}, f32[16,128,128]{2,1,0:T(8,128)}) custom-call(bf16[16384,2048]{1,0:T(8,128)(2,1)} %a_hbm.3, bf16[16,128,2048]{2,1,0:T(8,128)(2,1)} %broadcast_select_fusion.e_hbm, f32[1,2048]{1,0:T(1,128)} %bitcast.16, f32[16,128,128]{2,1,0:T(8,128)} %broadcast_in_dim.56.code_ref), custom_call_target="tpu_custom_call" | custom-call | tf_op jit(solution)/shard_map/forward/pallas_call | solution.py:250
  468.4 1.6 slice_reduce_fusion
  470.0 1.2 select_reduce_fusion
  471.2 0.7 pad_clamp_fusion
  471.8 8.1 gather_fusion.1
  480.0 592.3 %backward.1 = bf16[16,128,2048]{2,1,0:T(8,128)(2,1)} custom-call(bf16[16384,2048]{1,0:T(8,128)(2,1)} %a_hbm.3, bf16[16,128,2048]{2,1,0:T(8,128)(2,1)} %broadcast_select_fusion.e_hbm, f32[16,128,128]{2,1,0:T(8,128)} %get-tuple-element.6.cc_ref, f32[16,128,128]{2,1,0:T(8,128)} %broadcast_in_dim.56.code_ref), custom_call_target="tpu_custom_call" | custom-call | tf_op jit(solution)/shard_map/backward/pallas_call | solution.py:429
  1072.3 24.9 %bitcast_multiply_fusion = f32[2048,2048]{1,0:T(8,128)} fusion(bf16[16,128,2048]{2,1,0:T(8,128)(2,1)} %get-tuple-element.8, bf16[16384,2048]{1,0:T(8,128)(2,1)} %a_hbm.3, s32[]{:T(128)S(6)} %select_n.60, bf16[16,128,2048]{2,1,0:T(8,128)(2,1)} %backward.1), kind=kOutput, calls=%fused_computation.2 | convolution fusion | flops 16114515968 | bytes 41418756 | tf_op jit(solution)/shard_map/tbi,tbj->ij/dot_general | solution.py:473
  (2 shorter events, 0.0 us)
Async XLA Ops:
  1.3 47.9 %copy-start = (s32[128,16]{0,1:T(8,128)S(1)}, s32[128,16]{0,1:T(8,128)}, u32[]{:S(2)}) copy-start(s32[128,16]{0,1:T(8,128)} %param.8) | copy-start | bytes 24580
  49.3 7.6 copy-start.1

commit v2 on v1

--- a/solution.py
+++ b/solution.py
@@ -38,9 +38,9 @@
     return pltpu.make_async_remote_copy(src_ref=src, dst_ref=dst, send_sem=ssem, recv_sem=rsem, device_id=_dev(peer), device_id_type=MESH)
 
 
-def _fwd_kernel(n, steps, rows, nbuf, a_hbm, e_hbm, pi_ref, code_ref, al_hbm, x_hbm, cc_ref,
-                g, w, u, al, ebuf, tbuf, cs_send, cs_recv,
-                e_sem, w_sem, r_sem, out_sem, cs_ss, cs_rs, own_ss, own_rs, ici_ss, ici_rs, dd_ss, dd_rs):
+def _fwd_kernel(n, steps, rows, nbuf, a_hbm, e_hbm, e0_hbm, pi_ref, code_ref, sid_ref, al_hbm, a0_hbm, x_hbm, cc_ref, c0_ref,
+                g, w, u, al, ebuf, a0f, a0b, xi, tbuf, cs_send, cs_recv,
+                e_sem, w_sem, r_sem, out_sem, cs_ss, cs_rs, ici_ss, ici_rs, dd_ss, dd_rs):
     me, chip, core, partner, right, left = _place(n)
     chips = n // 2
     half = a_hbm.shape[0] // (2 * n)
@@ -70,13 +70,15 @@
     def e_copy(s):
         return pltpu.make_async_copy(e_hbm.at[s], ebuf.at[lax.rem(s, 2)], e_sem.at[lax.rem(s, 2)])
 
-    e_copy(jnp.int32(0)).start()
+    seqs = a0f.shape[0]
+    e0_copy = pltpu.make_async_copy(e0_hbm, a0b, e_sem.at[0])
+    e0_copy.start()
     for k in range(8):
         resident(k).start()
     for q in range(nbuf):
         stream(jnp.int32(q), q).start()
+    e_copy(jnp.int32(1)).start()
     tbuf[...] = jnp.zeros_like(tbuf)
-    u[...] = jnp.zeros_like(u)
     _barrier(me, n)
 
     def al_copy(s):
@@ -109,28 +111,8 @@
         ref = g.at[block(jnp.int32(1), 0, i)]
         return _remote(ref, ref, ici_ss.at[4 + i], ici_rs.at[4 + i], right if i == 0 else left)
 
-    def step(s, _):
-        e_copy(s).wait()
-
-        @pl.when(s + 1 < steps)
-        def _():
-            e_copy(s + 1).start()
-
-        @pl.when(s > 0)
-        def _():
-            al_copy(s - 1).wait()
-
-        code = code_ref[s]
-        init = (code > 0.5) & (code < 2.5)
-        part = jnp.zeros((rows, LANES), jnp.float32)
-        eb = ebuf.at[lax.rem(s, 2)]
-        for q in range(nq):
-            cols = slice(q * LANES, (q + 1) * LANES)
-            mass = jnp.where(init, jnp.broadcast_to(pi_ref[:, cols], (rows, LANES)), u[:, cols])
-            a = mass * eb[:, cols].astype(jnp.float32)
-            al[:, cols] = a
-            part = part + a
-        tbuf[0:rows, :] = part
+    def normalizer(part, count, meanwhile):
+        tbuf[0:count, :] = part
         row = jnp.sum(tbuf[...].T, axis=0, keepdims=True)
         cs_send[...] = jnp.broadcast_to(row, cs_send.shape)
         cs_recv[me] = jnp.broadcast_to(row, cs_send.shape)
@@ -139,33 +121,44 @@
             cp = _remote(cs_send, cs_recv.at[me], cs_ss.at[r - 1], cs_rs.at[r - 1], lax.rem(me + r, n))
             cp.start()
             cps.append(cp)
-
-        @pl.when(s > 0)
-        def _():
-            for h in range(2):
-                x_copy(s - 1, h).wait()
-
+        meanwhile()
         for cp in cps:
             cp.wait()
         crow = cs_recv[0]
         for r in range(1, n):
             crow = crow + cs_recv[r]
-        ccol = jnp.broadcast_to(crow[0:1, :], (LANES, LANES)).T[0:rows, :]
-        cc_ref[s] = ccol
-        live = code > 0.5
-        safe = jnp.where(live, ccol, 1.0)
-        for q in range(nq):
-            cols = slice(q * LANES, (q + 1) * LANES)
-            alpha = jnp.where(live, al[:, cols] / safe, 0.0)
-            al[:, cols] = alpha
-            h, o = divmod(q * LANES, half)
-            g[me * 2 + h, :, o:o + LANES] = alpha.astype(jnp.bfloat16)
-        al_copy(s).start()
-        for h in range(2):
-            x_copy(s, h).start()
-
-        @pl.when(s + 1 < steps)
-        def _():
+        return jnp.broadcast_to(crow[0:1, :], (LANES, LANES)).T[0:count, :]
+
+    lane = lax.broadcasted_iota(jnp.int32, (rows, LANES), 1).astype(jnp.float32)
+
+    def first_alphas(s):
+        pick = (sid_ref[s][:, 0:seqs] == lane[:, 0:seqs]).astype(jnp.bfloat16)
+        xi[...] = jnp.dot(pick, a0b[...], preferred_element_type=jnp.float32).astype(jnp.bfloat16)
+
+    e0_copy.wait()
+    part = jnp.zeros((seqs, LANES), jnp.float32)
+    for q in range(nq):
+        cols = slice(q * LANES, (q + 1) * LANES)
+        a = jnp.broadcast_to(pi_ref[:, cols], (seqs, LANES)) * a0b[:, cols].astype(jnp.float32)
+        a0f[:, cols] = a
+        part = part + a
+    c0 = normalizer(part, seqs, lambda: None)
+    c0_ref[...] = c0
+    for q in range(nq):
+        cols = slice(q * LANES, (q + 1) * LANES)
+        alpha = a0f[:, cols] / c0
+        a0f[:, cols] = alpha
+        a0b[:, cols] = alpha.astype(jnp.bfloat16)
+    a0_copy = pltpu.make_async_copy(a0f, a0_hbm, e_sem.at[0])
+    a0_copy.start()
+    first_alphas(0)
+    for h in range(2):
+        g[me * 2 + h] = xi[:, h * half:(h + 1) * half]
+        x_copy(0, h).start()
+    tbuf[...] = jnp.zeros_like(tbuf)
+
+    def exchange(s):
+        if True:
             sends = own_sends()
             for cp in sends:
                 cp.start()
@@ -233,16 +226,64 @@
                 for i in range(2):
                     dd(jnp.int32(j), jnp.int32(i), 2 * j + i).wait_send()
 
+    exchange(jnp.int32(0))
+    a0_copy.wait()
+
+    def step(s, _):
+        e_copy(s).wait()
+
+        @pl.when(s + 1 < steps)
+        def _():
+            e_copy(s + 1).start()
+
+        @pl.when(s > 1)
+        def _():
+            al_copy(s - 1).wait()
+
+        part = jnp.zeros((rows, LANES), jnp.float32)
+        eb = ebuf.at[lax.rem(s, 2)]
+        for q in range(nq):
+            cols = slice(q * LANES, (q + 1) * LANES)
+            a = u[:, cols] * eb[:, cols].astype(jnp.float32)
+            al[:, cols] = a
+            part = part + a
+
+        def meanwhile():
+            first_alphas(s)
+            for h in range(2):
+                x_copy(s - 1, h).wait()
+
+        ccol = normalizer(part, rows, meanwhile)
+        cc_ref[s] = ccol
+        live = code_ref[s] > 0.5
+        starts = sid_ref[s] > -0.5
+        safe = jnp.where(live, ccol, 1.0)
+        for q in range(nq):
+            cols = slice(q * LANES, (q + 1) * LANES)
+            alpha = jnp.where(live, al[:, cols] / safe, 0.0)
+            al[:, cols] = alpha
+            h, o = divmod(q * LANES, half)
+            x = jnp.where(starts, xi[:, cols].astype(jnp.float32), alpha)
+            g[me * 2 + h, :, o:o + LANES] = x.astype(jnp.bfloat16)
+        al_copy(s).start()
+        for h in range(2):
+            x_copy(s, h).start()
+
+        @pl.when(s + 1 < steps)
+        def _():
+            exchange(s)
+
         return 0
 
-    lax.fori_loop(0, steps, step, 0)
+    lax.fori_loop(1, steps, step, 0)
     al_copy(steps - 1).wait()
     for h in range(2):
         x_copy(steps - 1, h).wait()
 
 
-def _forward(n, a_loc, e_seq, init_loc, code):
+def _forward(n, cid, a_loc, e_seq, e_first, init_loc, code, sid):
     steps, rows, wide = e_seq.shape
+    seqs = e_first.shape[0]
     half = wide // 2
     nbuf = 4 if rows <= 80 else 2
     f32, bf16 = jnp.float32, jnp.bfloat16
@@ -251,28 +292,32 @@
         functools.partial(_fwd_kernel, n, steps, rows, nbuf),
         out_shape=(
             jax.ShapeDtypeStruct((steps, rows, wide), f32),
+            jax.ShapeDtypeStruct((seqs, wide), f32),
             jax.ShapeDtypeStruct((steps, rows, wide), bf16),
             jax.ShapeDtypeStruct((steps, rows, LANES), f32),
+            jax.ShapeDtypeStruct((seqs, LANES), f32),
         ),
-        in_specs=[ANY, ANY, VMEM, VMEM],
-        out_specs=(ANY, ANY, VMEM),
+        in_specs=[ANY, ANY, ANY, VMEM, VMEM, VMEM],
+        out_specs=(ANY, ANY, ANY, VMEM, VMEM),
         scratch_shapes=[
             pltpu.VMEM((2 * n, rows, half), bf16),
             pltpu.VMEM((8 + nbuf, half, wide), bf16),
             pltpu.VMEM((rows, wide), f32),
             pltpu.VMEM((rows, wide), f32),
             pltpu.VMEM((2, rows, wide), bf16),
+            pltpu.VMEM((seqs, wide), f32),
+            pltpu.VMEM((seqs, wide), bf16),
+            pltpu.VMEM((rows, wide), bf16),
             pltpu.VMEM((LANES, LANES), f32),
             pltpu.VMEM((8, LANES), f32),
             pltpu.VMEM((n, 8, LANES), f32),
             dma((2,)), dma((nbuf,)), dma((8,)), dma((3,)),
             dma((n - 1,)), dma((n - 1,)),
-            dma((2,)), dma((2,)),
             dma((6,)), dma((6,)), dma((8,)), dma((8,)),
         ],
-        compiler_params=pltpu.CompilerParams(collective_id=0, has_side_effects=True, vmem_limit_bytes=67043328),
+        compiler_params=pltpu.CompilerParams(collective_id=cid, has_side_effects=True, vmem_limit_bytes=67043328),
         name='forward',
-    )(a_loc, e_seq, init_loc, code)
+    )(a_loc, e_seq, e_first, init_loc, code, sid)
 
 
 def _bwd_kernel(n, steps, rows, nbuf, a_hbm, e_hbm, cc_ref, code_ref, w_hbm,
@@ -420,7 +465,7 @@
         ring(k, 0, right).wait_send()
 
 
-def _backward(n, a_loc, e_seq, ccol, code):
+def _backward(n, cid, a_loc, e_seq, ccol, code):
     steps, rows, wide = e_seq.shape
     half = wide // 2
     nbuf = 3 if rows <= 80 else 2
@@ -444,35 +489,72 @@
             dma((8,)), dma((8,)),
             dma((6,)), dma((2, 6)),
         ],
-        compiler_params=pltpu.CompilerParams(collective_id=1, has_side_effects=True, vmem_limit_bytes=67043328),
+        compiler_params=pltpu.CompilerParams(collective_id=cid, has_side_effects=True, vmem_limit_bytes=67043328),
         name='backward',
     )(a_loc, e_seq, ccol, code)
 
 
+def _ranks(lengths):
+    idx = jnp.arange(lengths.shape[0], dtype=jnp.int32)
+    ahead = (lengths[None, :] > lengths[:, None]) | ((lengths[None, :] == lengths[:, None]) & (idx[None, :] < idx[:, None]))
+    rank = jnp.sum(ahead.astype(jnp.int32), axis=1)
+    ordered = jnp.sum(jnp.where(rank[None, :] == idx[:, None], lengths[None, :], 0), axis=1)
+    return rank, ordered
+
+
+def _fits(ordered, slots, steps):
+    extra = ordered.shape[0] - slots
+    if extra == 0:
+        return jnp.bool_(True)
+    pair = ordered[slots:] + ordered[slots - extra:slots][::-1]
+    return jnp.max(pair) <= steps + 1
+
+
 def solution(mesh):
     n = mesh.shape['states']
 
     def local_run(trans_loc, emit_loc, init_loc, tokens_loc, lengths_loc):
-        rows, steps = tokens_loc.shape
+        seqs, steps = tokens_loc.shape
         wide = trans_loc.shape[1]
         group_idx = lax.axis_index('states')
-        pos = jnp.arange(steps, dtype=jnp.int32)[:, None]
-        tok = tokens_loc.T
-        init = pos == 0
-        live = pos < lengths_loc[None, :]
-        last = pos == lengths_loc[None, :] - 1
-        code = jnp.where(live, jnp.where(init, 1.0, 3.0) + jnp.where(last, 1.0, 0.0), 0.0)
-        code_b = jnp.broadcast_to(code[:, :, None], (steps, rows, LANES))
-        e_seq = jnp.transpose(jnp.take(emit_loc, tok, axis=1), (1, 2, 0))
-        al, xs, ccol = _forward(n, trans_loc, e_seq, init_loc[None, :], code_b)
-        ws = _backward(n, trans_loc, e_seq, ccol, code_b)
-        cc = ccol[:, :, 0]
-        loglik = jnp.sum(jnp.where(live, jnp.log(jnp.where(live, cc, 1.0)), 0.0), axis=0)
-        seq = jnp.arange(rows, dtype=jnp.int32)
-        posterior = al.reshape(steps * rows, wide)[(lengths_loc - 1) * rows + seq]
-        pair_sum = jnp.einsum('tbi,tbj->ij', xs[:-1], ws[1:], preferred_element_type=jnp.float32)
-        diag_block = lax.dynamic_slice_in_dim(trans_loc, group_idx * wide, wide, axis=0)
-        counts = diag_block.astype(jnp.float32) * pair_sum
-        return loglik, posterior, counts
+        rank, ordered = _ranks(lengths_loc)
+
+        def run(slots, cid):
+            first = rank < slots
+            slot = jnp.where(first, rank, 2 * slots - 1 - rank)
+            ahead = jnp.sum(jnp.where(rank[None, :] == slot[:, None], lengths_loc[None, :], 0), axis=1)
+            begin = jnp.where(first, 0, ahead - 1)
+            time = jnp.arange(steps, dtype=jnp.int32)
+            pos = time[None, :] - begin[:, None]
+            moves = (pos >= 1) & (pos < lengths_loc[:, None])
+            spread = (pos[:, :, None] == time[None, None, :]) & moves[:, :, None]
+            tok_at = jnp.sum(jnp.where(spread, tokens_loc[:, None, :], 0), axis=2)
+            here = slot[None, :] == jnp.arange(slots, dtype=jnp.int32)[:, None]
+            tok = jnp.sum(jnp.where(here[None] & moves.T[:, None, :], tok_at.T[:, None, :], 0), axis=2)
+            kind = jnp.where(moves, jnp.where(pos == lengths_loc[:, None] - 1, 4, 3), 0)
+            code = jnp.sum(jnp.where(here[None], kind.T[:, None, :], 0), axis=2)
+            later = (pos == 0) & ~(first & (lengths_loc == 1) & (rank >= 2 * slots - seqs))[:, None]
+            number = jnp.arange(seqs, dtype=jnp.int32) + 1
+            sid = jnp.sum(jnp.where(here[None] & later.T[:, None, :], number[None, None, :], 0), axis=2) - 1
+            code_b = jnp.broadcast_to(code.astype(jnp.float32)[:, :, None], (steps, slots, LANES))
+            sid_b = jnp.broadcast_to(sid.astype(jnp.float32)[:, :, None], (steps, slots, LANES))
+            look = jnp.concatenate([tok.reshape(-1), tokens_loc[:, 0]])
+            picked = jnp.take(emit_loc, look, axis=1, mode='clip').T
+            e_seq = picked[:steps * slots].reshape(steps, slots, wide)
+            e_first = picked[steps * slots:]
+            al, a0, xs, ccol, c0 = _forward(n, cid, trans_loc, e_seq, e_first, init_loc[None, :], code_b, sid_b)
+            ws = _backward(n, cid + 1, trans_loc, e_seq, ccol, code_b)
+            logs = jnp.where(code > 0, jnp.log(jnp.where(code > 0, ccol[:, :, 0], 1.0)), 0.0)
+            mine = jnp.sum(jnp.where(here[None], logs[:, :, None], 0.0), axis=1)
+            loglik = jnp.log(c0[:, 0]) + jnp.sum(jnp.where(moves.T, mine, 0.0), axis=0)
+            end = (begin + lengths_loc - 1) * slots + slot
+            posterior = jnp.where((lengths_loc == 1)[:, None], a0, jnp.take(al.reshape(steps * slots, wide), end, axis=0, mode='clip'))
+            pair_sum = jnp.einsum('tbi,tbj->ij', xs[:-1], ws[1:], preferred_element_type=jnp.float32)
+            diag_block = lax.dynamic_slice_in_dim(trans_loc, group_idx * wide, wide, axis=0)
+            counts = diag_block.astype(jnp.float32) * pair_sum
+            return loglik, posterior, counts
+
+        few = seqs * 5 // 8
+        return lax.cond(_fits(ordered, few, steps), lambda: run(few, 0), lambda: run(seqs, 2))
 
     return jax.shard_map(local_run, mesh=mesh, in_specs=(P(None, 'states'), P('states', None), P('states'), P('seqs', None), P('seqs')), out_specs=(P('seqs'), P('seqs', 'states'), P(('seqs', 'states'), None)), check_vma=False)

time: 1100 us -> 835 us (0.76)
  Pallas kernels: 1000 us -> 735 us
  local copies, waits for them, and re-layouts: 59.1 us -> 43.1 us
    pallas_call x1, Pallas kernels: 592 us -> 407 us  [_backward(): pl.pallas_call(functools.partial(_bwd_kernel, n, steps, rows, nbuf), out_...]
    pallas_call x1, Pallas kernels: 409 us -> 328 us  [_forward(): pl.pallas_call(functools.partial(_fwd_kernel, n, steps, rows, nbuf), out_...]
    gather x2, local copies, waits for them, and re-layouts: 56.1 us -> 31 us  [the longest x1 25.6 us: run(): picked = jnp.take(emit_loc, look, axis=1, mode='clip').T]
where the time goes in v2:
time: 835 us; the launch traced here: 825 us
  Pallas kernels  735 us (88%)
  local copies, waits for them, and re-layouts  43.1 us (5%)
  matrix products  19.2 us (2%)
  other arithmetic  15.4 us (2%)
  loops' own time  9.36 us (1%)
    pallas_call x1, Pallas kernels, _backward(): pl.pallas_call(functools.partial(_bwd_kernel, n, steps, rows, nbuf), out_...  407 us
    pallas_call x1, Pallas kernels, _forward(): pl.pallas_call(functools.partial(_fwd_kernel, n, steps, rows, nbuf), out_...  328 us
    gather x1, local copies, waits for them, and re-layouts, run(): picked = jnp.take(emit_loc, look, axis=1, mode='clip').T  25.6 us
    dot_general x1, matrix products, run(): jnp.einsum('tbi,tbj->ij', xs[:-1], ws[1:], preferred_element_type=jnp.flo...  19.2 us

profile of v2, /device:TPU:112, one launch (start us, length us, event | category | flops | bytes accessed | tf_op | source)
XLA Modules:
  0.0 825.3 jit_solution(14052080247257699375)
XLA Ops:
  0.6 0.9 convert_reduce_fusion
  1.5 0.8 select_reduce_fusion.16
  2.5 0.7 add_reduce_fusion
  3.8 820.0 %conditional.1 = (f32[128]{0:T(128)}, f32[128,2048]{1,0:T(8,128)}, f32[2048,2048]{1,0:T(8,128)}) conditional(s32[]{:T(128)} %convert_element_type.41, (s32[128]{0:T(128)S(1)}, s32[128]{0:T(128)}, s32[128,16]{0,1:T(8,128)}, bf16[2048,10000]{0,1:T(8,128)(2,1)}, f32[2048]{0:T(1024)}, /*index=5*/bf16[16384,2048]{1,0:T(8,128)(2,1)}, ...), branch_computations={%region_3.11_spmd, %region_11.19_spmd} | conditional | flops 16117656576 | bytes 89026264 | solution.py:558
  13.5 0.8 select_reduce_fusion.14
  14.3 1.3 multiply_add_fusion.1
  15.6 1.1 broadcast_compare_fusion.1
  18.8 0.7 select_reduce_fusion.13
  19.5 0.9 select_reduce_fusion.10
  20.5 25.6 %gather_fusion.2 = bf16[1408,2048]{1,0:T(8,128)(2,1)} fusion(bf16[2048,10000]{0,1:T(8,128)(2,1)} %get-tuple-element.69, s32[2048]{0:T(1024)S(1)} %pad_clamp_fusion.2), kind=kCustom, calls=%fused_computation.2 | custom fusion | bytes 11539968 | tf_op jit(solution)/shard_map/cond/branch_1_fun/jit(_take)/gather | solution.py:542
  46.1 5.7 slice.60
  51.9 1.9 slice.61.e0_hbm
  53.7 1.1 broadcast_in_dim.316.code_ref
  54.8 1.1 broadcast_in_dim.318.sid_ref
  55.9 328.2 %forward.3 = (f32[16,80,2048]{2,1,0:T(8,128)}, f32[128,2048]{1,0:T(8,128)}, bf16[16,80,2048]{2,1,0:T(8,128)(2,1)}, f32[16,80,128]{2,1,0:T(8,128)}, f32[128,128]{1,0:T(8,128)}) custom-call(bf16[16384,2048]{1,0:T(8,128)(2,1)} %get-tuple-element.73.a_hbm, bf16[16,80,2048]{2,1,0:T(8,128)(2,1)} %bitcast.25, bf16[128,2048]{1,0:T(8,128)(2,1)} %slice.61.e0_hbm, ...), custom_call_target="tpu_custom_call" | custom-call | tf_op jit(solution)/shard_map/cond/branch_1_fun/forward/pallas_call | solution.py:291
  384.2 1.0 log_reduce_fusion.1
  385.2 0.7 compare_bitcast_fusion.1
  386.3 1.4 select_reduce_fusion.9
  387.7 0.9 select_reduce_fusion.8
  388.7 0.7 select_reduce_fusion.15
  390.6 5.4 gather_fusion.3
  396.0 1.1 broadcast_select_fusion.1
  397.1 407.2 %backward.3 = bf16[16,80,2048]{2,1,0:T(8,128)(2,1)} custom-call(bf16[16384,2048]{1,0:T(8,128)(2,1)} %get-tuple-element.73.a_hbm, bf16[16,80,2048]{2,1,0:T(8,128)(2,1)} %bitcast.26, f32[16,80,128]{2,1,0:T(8,128)} %get-tuple-element.47.cc_ref, f32[16,80,128]{2,1,0:T(8,128)} %broadcast_in_dim.316.code_ref), custom_call_target="tpu_custom_call" | custom-call | tf_op jit(solution)/shard_map/cond/branch_1_fun/backward/pallas_call | solution.py:474
  804.4 19.2 %bitcast_multiply_fusion.1 = f32[2048,2048]{1,0:T(8,128)} fusion(bf16[16,80,2048]{2,1,0:T(8,128)(2,1)} %get-tuple-element.51, bf16[16384,2048]{1,0:T(8,128)(2,1)} %get-tuple-element.73.a_hbm, s32[]{:T(128)S(6)} %select_n.132, bf16[16,80,2048]{2,1,0:T(8,128)(2,1)} %backward.3), kind=kOutput, calls=%fused_computation.42 | convolution fusion | flops 10074718208 | bytes 35323908 | tf_op jit(solution)/shard_map/cond/branch_1_fun/tbi,tbj->ij/dot_general | solution.py:552
  (28 shorter events, 4.5 us)
Async XLA Ops:
  15.6 3.9 copy-start.6
  17.4 2.1 copy-start.3
  20.4 33.3 %copy-start.4 = (s32[16,80]{1,0:T(8,128)}, s32[16,80]{1,0:T(8,128)S(1)}, u32[]{:S(2)}) copy-start(s32[16,80]{1,0:T(8,128)S(1)} %get-tuple-element.78) | copy-start | bytes 15364 | tf_op jit(solution)/shard_map/cond
  384.1 11.9 %copy-start.1 = (f32[128,2048]{1,0:T(8,128)S(1)}, f32[128,2048]{1,0:T(8,128)}, u32[]{:S(2)}) copy-start(f32[128,2048]{1,0:T(8,128)} %get-tuple-element.48) | copy-start | bytes 3145732 | tf_op jit(solution)/shard_map/cond
  384.1 11.9 %copy-start.8 = (pred[128]{0:T(512)(128)(4,1)S(1)}, pred[128]{0:T(512)(128)(4,1)}, u32[]{:S(2)}) copy-start(pred[128]{0:T(512)(128)(4,1)} %get-tuple-element.89) | copy-start | bytes 388 | tf_op jit(solution)/shard_map/cond
